TPU v7x, 32 devices: a whole 2x2x4 slice. The times are simulated.
32 devices in a mesh: rep: 1, dp: 32 (over x, y, z, core).
Axes of the slice: x: 2, y: 2, z: 4, core: 2. Of those that a mesh axis runs over, the one named last changes fastest.
Arguments:
- g_w_gate: bfloat16 [32, 2, 1536, 4224], P(('rep', 'dp'))
- g_w_up: bfloat16 [32, 2, 1536, 4224], P(('rep', 'dp'))
- g_w_down: bfloat16 [32, 2, 4224, 1536], P(('rep', 'dp'))
- w_gate: bfloat16 [2, 1536, 4224], replicated
- w_up: bfloat16 [2, 1536, 4224], replicated
- w_down: bfloat16 [2, 4224, 1536], replicated
- m_w_gate: float32 [2, 1536, 4224], P(None, 'dp')
- m_w_up: float32 [2, 1536, 4224], P(None, 'dp')
- m_w_down: float32 [2, 4224, 1536], P(None, 'dp')
- v_w_gate: float32 [2, 1536, 4224], P(None, 'dp')
- v_w_up: float32 [2, 1536, 4224], P(None, 'dp')
- v_w_down: float32 [2, 4224, 1536], P(None, 'dp')
Outputs:
- output 1: bfloat16 [2, 1536, 4224], P('rep')
- output 2: bfloat16 [2, 1536, 4224], P('rep')
- output 3: bfloat16 [2, 4224, 1536], P('rep')
- output 4: float32 [2, 1536, 4224], P('rep', 'dp')
- output 5: float32 [2, 1536, 4224], P('rep', 'dp')
- output 6: float32 [2, 4224, 1536], P('rep', 'dp')
- output 7: float32 [2, 1536, 4224], P('rep', 'dp')
- output 8: float32 [2, 1536, 4224], P('rep', 'dp')
- output 9: float32 [2, 4224, 1536], P('rep', 'dp')
All inputs are finite; a program needn't handle non-finite values.
Results may differ from a plain program's by a relative error of at most 0.022.
Values are sent between devices in bfloat16 or wider.
A program may use at most 2 GiB of HBM per device.

v0:
```python
import jax
import jax.numpy as jnp
from jax import lax
from jax.sharding import PartitionSpec as P


def adamw(w, m, v, g):
    m = 0.9 * m + 0.1 * g
    v = 0.95 * v + 0.05 * g * g
    step = m * lax.rsqrt(v + 1e-8) + 0.1 * w
    return (w - 0.02 * step).astype(jnp.bfloat16), m, v


def solution(mesh):
    def step(*arrays):
        terms, weights, m, v = (arrays[i : i + 3] for i in (0, 3, 6, 9))
        gradients = [lax.psum_scatter(t[0], "dp", scatter_dimension=1, tiled=True).astype(jnp.float32) for t in terms]
        me = lax.axis_index("dp")
        own = [lax.dynamic_slice_in_dim(w, me * one.shape[1], one.shape[1], 1).astype(jnp.float32) for w, one in zip(weights, m, strict=True)]
        new = [adamw(w, m, v, g) for w, m, v, g in zip(own, m, v, gradients, strict=True)]
        whole = [lax.all_gather(one[0], "dp", axis=1, tiled=True) for one in new]
        return (*whole, *(one[1] for one in new), *(one[2] for one in new))

    all_of, cut = P(None, None, None), P(None, "dp", None)
    return jax.shard_map(
        step,
        mesh=mesh,
        in_specs=(P(("rep", "dp"), None, None, None),) * 3 + (all_of,) * 3 + (cut,) * 6,
        out_specs=(P("rep", None, None),) * 3 + (P("rep", "dp", None),) * 6,
        check_vma=False,
    )
```

profile of v0, /device:TPU:0, one launch (start us, length us, event | category | flops | bytes accessed | tf_op | source)
XLA Modules:
  0.0 1550.2 jit_solution(13535946689243359681)
XLA Ops:
  7.2 0.0 all-reduce.3.cloned.1.call-start
  7.2 114.8 %copy.30 = bf16[1,2,4224,1536]{3,1,2,0:T(2,128)(2,1)} copy(bf16[1,2,4224,1536]{3,2,1,0:T(8,128)(2,1)} %param.14) | data formatting | bytes 51904512 | tf_op args[2]
  122.0 0.0 all-reduce.3.cloned.1.call-update
  122.0 0.0 reduce-scatter.5.cloned.1.call-start
  122.1 0.7 reduce-scatter.5.cloned.1.call-update
  122.8 0.0 reduce-scatter.3.cloned.1.call-start
  122.8 0.7 reduce-scatter.3.cloned.1.call-update
  123.5 0.0 copy-start.1
  123.5 0.0 all-gather.8.cloned.1.call-start
  123.6 1.5 constant_dynamic-slice_fusion
  125.1 400.2 %all-reduce.3.cloned.1.call-done = bf16[2,4224,1536]{2,0,1:T(2,128)(2,1)} async-done(((bf16[2,4224,1536]{2,0,1:T(2,128)(2,1)}), bf16[2,4224,1536]{2,0,1:T(2,128)(2,1)}) %all-reduce.3.cloned.1.call-update) | async-done | bytes 25952272
  525.3 0.0 copy-done.1
  525.3 7.6 fusion.14
  532.8 0.0 all-gather.8.cloned.1.call-update
  532.9 0.0 all-gather.6.cloned.1.call-start
  532.9 244.8 %reduce-scatter.5.cloned.1.call-done = bf16[2,48,4224]{2,1,0:T(8,128)(2,1)} async-done(((bf16[2,1536,4224]{2,1,0:T(8,128)(2,1)}), bf16[2,48,4224]{2,1,0:T(8,128)(2,1)}) %reduce-scatter.5.cloned.1.call-update) | async-done | bytes 811024 | tf_op jit(solution)/shard_map/reduce_scatter | solution.py:17
  777.7 0.0 copy-start.2
  777.7 4.9 fusion.6
  782.6 0.0 all-gather.6.cloned.1.call-update
  782.6 0.0 all-gather.4.cloned.1.call-start
  782.7 247.2 %reduce-scatter.3.cloned.1.call-done = bf16[2,48,4224]{2,1,0:T(8,128)(2,1)} async-done(((bf16[2,1536,4224]{2,1,0:T(8,128)(2,1)}), bf16[2,48,4224]{2,1,0:T(8,128)(2,1)}) %reduce-scatter.3.cloned.1.call-update) | async-done | bytes 811024 | tf_op jit(solution)/shard_map/reduce_scatter | solution.py:17
  1029.8 0.0 copy-done.2
  1029.8 0.0 copy-done.3
  1029.8 3.7 fusion.2
  1033.6 0.0 all-gather.4.cloned.1.call-update
  1033.6 156.4 %all-gather.8.cloned.1.call-done = bf16[2,4224,1536]{2,0,1:T(2,128)(2,1)} async-done(((bf16[2,132,1536]{2,0,1:T(2,128)(2,1)}), bf16[2,4224,1536]{2,0,1:T(2,128)(2,1)}) %all-gather.8.cloned.1.call-update) | async-done | bytes 25952272 | tf_op jit(solution)/shard_map/all_gather | solution.py:21
  1190.0 24.0 %copy.26 = bf16[2,4224,1536]{2,1,0:T(8,128)(2,1)} copy(bf16[2,4224,1536]{2,0,1:T(2,128)(2,1)} %all-gather.8.cloned.1.call-done) | data formatting | bytes 51904512
  1214.0 135.4 %all-gather.6.cloned.1.call-done = bf16[2,1536,4224]{2,1,0:T(8,128)(2,1)} async-done(((bf16[2,48,4224]{2,1,0:T(8,128)(2,1)}), bf16[2,1536,4224]{2,1,0:T(8,128)(2,1)}) %all-gather.6.cloned.1.call-update) | async-done | bytes 25952272 | tf_op jit(solution)/shard_map/all_gather | solution.py:21
  1349.3 159.3 %all-gather.4.cloned.1.call-done = bf16[2,1536,4224]{2,1,0:T(8,128)(2,1)} async-done(((bf16[2,48,4224]{2,1,0:T(8,128)(2,1)}), bf16[2,1536,4224]{2,1,0:T(8,128)(2,1)}) %all-gather.4.cloned.1.call-update) | async-done | bytes 25952272 | tf_op jit(solution)/shard_map/all_gather | solution.py:21
  1508.7 22.2 %copy.34 = bf16[2,1536,4224]{2,1,0:T(8,128)(2,1)} copy(bf16[2,1536,4224]{2,1,0:T(8,128)(2,1)} %all-gather.4.cloned.1.call-done) | data formatting | bytes 51904512
  1530.9 3.3 copy-done
  1534.2 9.2 copy.35
  (2 shorter events, 0.0 us)
Async XLA Ops:
  7.2 518.1 %all-reduce.3.cloned.1.call-start = ((), (), s32[]{:S(2)}) async-start(), calls=%async_computation.7 | async-start | bytes 51904512
  122.0 655.7 %reduce-scatter.5.cloned.1.call-start = ((), (), s32[]{:S(2)}) async-start(), calls=%async_computation.4 | async-start | bytes 26763264 | tf_op jit(solution)/shard_map/reduce_scatter | solution.py:17
  122.8 907.1 %reduce-scatter.3.cloned.1.call-start = ((), (), s32[]{:S(2)}) async-start(), calls=%async_computation.2 | async-start | bytes 26763264 | tf_op jit(solution)/shard_map/reduce_scatter | solution.py:17
  123.5 401.8 %copy-start.1 = (f32[2,132,1536]{2,0,1:T(2,128)S(1)}, f32[2,132,1536]{2,0,1:T(2,128)}, u32[]{:S(2)}) copy-start(f32[2,132,1536]{2,0,1:T(2,128)} %param.23) | copy-start | bytes 4866052
  123.5 1066.5 %all-gather.8.cloned.1.call-start = ((), (), s32[]{:S(2)}) async-start(), calls=%async_computation.6 | async-start | bytes 26763264 | tf_op jit(solution)/shard_map/all_gather | solution.py:21
  532.9 816.5 %all-gather.6.cloned.1.call-start = ((), (), s32[]{:S(2)}) async-start(), calls=%async_computation.5 | async-start | bytes 26763264 | tf_op jit(solution)/shard_map/all_gather | solution.py:21
  777.7 252.1 %copy-start.2 = (f32[2,48,4224]{2,1,0:T(8,128)S(1)}, f32[2,48,4224]{2,1,0:T(8,128)}, u32[]{:S(2)}) copy-start(f32[2,48,4224]{2,1,0:T(8,128)} %param.21) | copy-start | bytes 4866052
  777.7 252.1 %copy-start.3 = (f32[2,48,4224]{2,1,0:T(8,128)S(1)}, f32[2,48,4224]{2,1,0:T(8,128)}, u32[]{:S(2)}) copy-start(f32[2,48,4224]{2,1,0:T(8,128)} %param.18) | copy-start | bytes 4866052
  782.6 726.0 %all-gather.4.cloned.1.call-start = ((), (), s32[]{:S(2)}) async-start(), calls=%async_computation.3 | async-start | bytes 26763264 | tf_op jit(solution)/shard_map/all_gather | solution.py:21
  1508.7 25.5 %copy-start = (bf16[2,1536,4224]{2,1,0:T(8,128)(2,1)S(1)}, bf16[2,1536,4224]{2,1,0:T(8,128)(2,1)}, u32[]{:S(2)}) copy-start(bf16[2,1536,4224]{2,1,0:T(8,128)(2,1)} %all-gather.6.cloned.1.call-done) | copy-start | bytes 77856768
Sparse Core Ops, SparseCore 0:
  122.1 403.0 all-reduce.2
  531.7 245.9 reduce-scatter.4
  784.1 245.6 reduce-scatter.2
  1033.3 156.6 all-gather.7
  1193.5 155.8 all-gather.5
  1352.8 155.8 all-gather.3
where the time goes:
time: 1550 us
  waiting for transfers between devices  1340 us (86%)
  local copies, waits for them, and re-layouts  175 us (11%)
  other arithmetic  16.2 us (1%)
    reduce_scatter x2, waiting for transfers between devices, step(): lax.psum_scatter(t[0], 'dp', scatter_dimension=1, tiled=True)  492 us
    all_gather x3, waiting for transfers between devices, step(): whole = [lax.all_gather(one[0], 'dp', axis=1, tiled=True) for one in new]  451 us
    unnamed x7, waiting for transfers between devices  402 us
    unnamed x12, local copies, waits for them, and re-layouts  173 us
  transfers between devices with their start and end apart: 6, of which 6 were waited for; matrix products, arithmetic and copies ran while one was open for 3% of the time, Pallas kernels for 0%

commit v1 on v0

v1 whole, which is shorter than its diff:
```python
import functools

import jax
import jax.numpy as jnp
from jax import lax
from jax.experimental import pallas as pl
from jax.experimental.pallas import tpu as pltpu
from jax.sharding import PartitionSpec as P

MESH = pl.DeviceIdType.MESH
F32, BF16 = jnp.float32, jnp.bfloat16
TILES = 198
T = 33
PAIRS = 3 * 2 * TILES // T // 2
EACH = PAIRS // 3
SLOTS = 4
X, Y, ZL, ZH = range(4)
WEIGHT = (8, 4, 1, 2)
ORDER = ((X, ZL, Y, ZH), (Y, ZL, X, ZH))


class Place:
    def __init__(self):
        me = lax.axis_index("dp")
        self.core = lax.rem(me, 2)
        self.chip = lax.div(me, 2)
        z = lax.rem(self.chip, 4)
        self.bit = {X: lax.div(me, 16), Y: lax.rem(lax.div(me, 8), 2), ZL: lax.rem(z, 2), ZH: lax.div(z, 2)}
        self.peer = me + 1 - 2 * self.core
        self.partner = {b: me + 2 * WEIGHT[b] * (1 - 2 * self.bit[b]) for b in range(4)}

    def greet(self):
        barrier = pltpu.get_barrier_semaphore()
        for other in (self.peer, *self.partner.values()):
            pl.semaphore_signal(barrier, inc=1, device_id={"dp": other}, device_id_type=MESH)
        pl.semaphore_wait(barrier, 5)


def when(condition):
    return pl.when(condition)


def send(src, dst, sems, at, device):
    send_sem, recv_sem = sems
    return pltpu.make_async_remote_copy(
        src_ref=src, dst_ref=dst, send_sem=send_sem.at[at], recv_sem=recv_sem.at[at], device_id={"dp": device}, device_id_type=MESH
    )


def for_chunk(i, colour, core, act):
    k = 2 * lax.rem(i, EACH) + colour
    per = TILES // T
    for which in range(3):

        @pl.when(lax.div(i, EACH) == which)
        def _():
            if which < 2:
                act(which, lax.div(k, per), lax.rem(k, per) * T)
            else:
                act(which, core, k * T)


def sum_kernel(gg, gu, gd, md, vd, og, ou, od, mp, vp, own, cor, s1, r1, s2, r2, s3, r3, s4, r4, a1, a2, a3, res, load_sem, ssem, rsem, out_sem, xs, xr, ms, mr):
    at = Place()
    core, bit = at.core, at.bit
    at.greet()
    sems = (ssem, rsem)

    moments = [send(src.at[1 - core], dst, (ms, mr), n, at.peer) for n, (src, dst) in enumerate(((md, mp), (vd, vp)))]
    for copy in moments:
        copy.start()

    def slot(i):
        return lax.rem(i, SLOTS)

    def fetch(i, colour):
        s = slot(i)
        mine, theirs = own.at[colour, s], cor.at[colour, s]
        raw = send(mine, theirs, sems, (0, colour, s), at.peer)
        pl.when(i >= SLOTS)(raw.wait_send)

        def act(which, layer, first):
            if which < 2:
                g = (gg, gu)[which]
                a, b = g.at[layer, :, core, pl.ds(first, T)], g.at[layer, :, 1 - core, pl.ds(first, T)]
            else:
                a, b = gd.at[core, :, pl.ds(first, T)], gd.at[1 - core, :, pl.ds(first, T)]
            send(b, theirs, sems, (0, colour, s), at.peer).start()
            pltpu.make_async_copy(a, mine, load_sem.at[colour, s]).start()

        for_chunk(i, colour, core, act)

    def exchange(stage, i, colour, src, dst):
        s = slot(i)
        return send(src.at[colour, s], dst.at[colour, s], sems, (stage, colour, s), at.partner[ORDER[colour][stage - 1]])

    def block(colour, first_bits, j, free):
        q = 0
        for b, v in zip(ORDER[colour], first_bits):
            q = q + WEIGHT[b] * v
        for n, b in enumerate(ORDER[colour][4 - free :]):
            q = q + WEIGHT[b] * lax.rem(lax.div(j, 2 ** (free - 1 - n)), 2)
        return q

    def f32(ref):
        return ref[...].astype(F32)

    def first(i, colour):
        s = slot(i)
        pltpu.make_async_copy(own.at[colour, s], own.at[colour, s], load_sem.at[colour, s]).wait()
        send(own.at[colour, s], cor.at[colour, s], sems, (0, colour, s), at.peer).wait_recv()
        out = exchange(1, i, colour, s1, r1)
        pl.when(i >= SLOTS)(out.wait_send)
        b1 = ORDER[colour][0]

        def body(j, _):
            q = block(colour, (1 - bit[b1],), j, 3)
            s1[colour, s, j] = (f32(own.at[colour, s, q]) + f32(cor.at[colour, s, q])).astype(BF16)
            return 0

        lax.fori_loop(0, 8, body, 0)
        out.start()

    def second(i, colour):
        s = slot(i)
        exchange(1, i, colour, s1, r1).wait_recv()
        out = exchange(2, i, colour, s2, r2)
        pl.when(i >= SLOTS)(out.wait_send)
        b1, b2 = ORDER[colour][:2]

        def total(j, v):
            q = block(colour, (bit[b1], v), j, 2)
            return f32(own.at[colour, s, q]) + f32(cor.at[colour, s, q]) + f32(r1.at[colour, s, v * 4 + j])

        def give(j, _):
            s2[colour, s, j] = total(j, 1 - bit[b2]).astype(BF16)
            return 0

        def keep(j, _):
            a1[colour, lax.rem(i, 2), j] = total(j, bit[b2])
            return 0

        lax.fori_loop(0, 4, give, 0)
        out.start()
        lax.fori_loop(0, 4, keep, 0)

    def third(i, colour):
        s = slot(i)
        exchange(2, i, colour, s2, r2).wait_recv()
        out = exchange(3, i, colour, s3, r3)
        pl.when(i >= SLOTS)(out.wait_send)
        v = bit[ORDER[colour][2]]

        def give(j, _):
            n = (1 - v) * 2 + j
            s3[colour, s, j] = (a1[colour, lax.rem(i, 2), n] + f32(r2.at[colour, s, n])).astype(BF16)
            return 0

        def keep(j, _):
            n = v * 2 + j
            a2[colour, lax.rem(i, 2), j] = a1[colour, lax.rem(i, 2), n] + f32(r2.at[colour, s, n])
            return 0

        lax.fori_loop(0, 2, give, 0)
        out.start()
        lax.fori_loop(0, 2, keep, 0)

    def fourth(i, colour):
        s = slot(i)
        exchange(3, i, colour, s3, r3).wait_recv()
        out = exchange(4, i, colour, s4, r4)
        pl.when(i >= SLOTS)(out.wait_send)
        v = bit[ORDER[colour][3]]
        s4[colour, s] = (a2[colour, lax.rem(i, 2), 1 - v] + f32(r3.at[colour, s, 1 - v])).astype(BF16)
        out.start()
        a3[colour, lax.rem(i, 2)] = a2[colour, lax.rem(i, 2), v] + f32(r3.at[colour, s, v])

    def result(colour, s, which, layer, first):
        dst = (og, ou, od)[which].at[layer, pl.ds(first, T)]
        return pltpu.make_async_copy(res.at[colour, s], dst, out_sem.at[colour, s])

    def share(i, colour, first):
        return send(res.at[colour, slot(i)], od.at[core, pl.ds(first, T)], (xs, xr), (colour, i - 2 * EACH), at.peer)

    def fifth(i, colour):
        s = slot(i)
        exchange(4, i, colour, s4, r4).wait_recv()
        pl.when(i >= SLOTS)(result(colour, s, 0, 0, 0).wait)

        @pl.when(i >= SLOTS + 2 * EACH)
        def _():
            share(i - SLOTS, colour, 0).wait_send()

        res[colour, s] = (a3[colour, lax.rem(i, 2)] + f32(r4.at[colour, s])).astype(BF16)

        def act(which, layer, first):
            result(colour, s, which, layer, first).start()
            if which == 2:
                share(i, colour, first).start()

        for_chunk(i, colour, core, act)

    for colour in range(2):
        fetch(0, colour)

    def step(i, _):
        @pl.when(i < PAIRS)
        def _():
            for colour in range(2):
                first(i, colour)

        @pl.when(i + 1 < PAIRS)
        def _():
            for colour in range(2):
                fetch(i + 1, colour)

        for late, stage in enumerate((second, third, fourth, fifth), 1):

            @pl.when((i >= late) & (i < PAIRS + late))
            def _():
                for colour in range(2):
                    stage(i - late, colour)

        return 0

    lax.fori_loop(0, PAIRS + 4, step, 0)
    for colour in range(2):
        for s in range(SLOTS):
            send(own.at[colour, s], cor.at[colour, s], sems, (0, colour, s), at.peer).wait_send()
            for stage, (src, dst) in enumerate(((s1, r1), (s2, r2), (s3, r3), (s4, r4)), 1):
                exchange(stage, s, colour, src, dst).wait_send()
            result(colour, s, 0, 0, 0).wait()
            share(PAIRS - SLOTS + s, colour, 0).wait_send()
        for i in range(2 * EACH, PAIRS):
            share(i, colour, 0).wait_recv()
    for copy in moments:
        copy.wait_send()
        copy.wait_recv()


def gather_kernel(wg, wu, wd, og, ou, od, load_sem, ssem, rsem):
    at = Place()
    core, bit, chip = at.core, at.bit, at.chip
    at.greet()
    sems = (ssem, rsem)

    def some(which, layer, first, q):
        return od.at[layer, q, pl.ds(first, T)] if which == 2 else (og, ou)[which].at[layer, q, core, pl.ds(first, T)]

    def mine(which, layer, first):
        return wd.at[pl.ds(first, T)] if which == 2 else (wg, wu)[which].at[layer, pl.ds(first, T)]

    def sized(n, stage, s, colour):
        dst = some(0, 0, 0, pl.ds(0, n))
        return send(dst, dst, sems, (stage, colour, s), at.peer)

    def local(which, layer, first, colour, s):
        return pltpu.make_async_copy(mine(which, layer, first), some(which, layer, first, chip), load_sem.at[colour, s])

    def go(stage, i, colour):
        s = lax.rem(i, SLOTS)
        if stage:
            sized(2 ** (stage - 1), stage - 1, s, colour).wait_recv()
        pl.when(i >= SLOTS)(sized(2**stage, stage, s, colour).wait_send)
        if stage == 1:
            local(0, 0, 0, colour, s).wait()

        def act(which, layer, first):
            if stage == 0:
                local(which, layer, first, colour, s).start()
                send(mine(which, layer, first), some(which, layer, first, chip), sems, (0, colour, s), at.partner[ZH]).start()
            elif stage == 4:
                every = some(which, layer, first, slice(None))
                send(every, every, sems, (4, colour, s), at.peer).start()
            else:
                free = ORDER[colour][4 - stage :]
                for n in range(2**stage):
                    q = chip
                    for m, b in enumerate(free):
                        q = q + WEIGHT[b] * ((n >> m & 1) - bit[b])
                    part = some(which, layer, first, q)
                    send(part, part, sems, (stage, colour, s), at.partner[ORDER[colour][3 - stage]]).start()

        for_chunk(i, colour, core, act)

    def step(i, _):
        for stage in range(5):

            @pl.when((i >= stage) & (i < PAIRS + stage))
            def _():
                for colour in range(2):
                    go(stage, i - stage, colour)

        @pl.when(i >= 5)
        def _():
            for colour in range(2):
                sized(16, 4, lax.rem(i - 5, SLOTS), colour).wait_recv()

        return 0

    lax.fori_loop(0, PAIRS + 5, step, 0)
    for colour in range(2):
        for s in range(SLOTS):
            for stage in range(5):
                sized(2**stage, stage, s, colour).wait_send()


def summed(gg, gu, gd, md, vd):
    any_ = pl.BlockSpec(memory_space=pl.ANY)
    shape = lambda s, d=BF16: jax.ShapeDtypeStruct(s, d)
    vmem = lambda n, k=SLOTS: pltpu.VMEM((2, k, n, T, 8, 128), BF16)
    dma = lambda *s: pltpu.SemaphoreType.DMA(s)
    return pl.pallas_call(
        sum_kernel,
        name="sums",
        out_shape=[shape((2, TILES, 8, 128)), shape((2, TILES, 8, 128)), shape((2, 2 * TILES, 8, 128))] + [shape(md.shape[1:], F32)] * 2,
        in_specs=[any_] * 5,
        out_specs=[any_] * 5,
        scratch_shapes=[
            vmem(16), vmem(16), vmem(8), vmem(8), vmem(4), vmem(4), vmem(2), vmem(2),
            pltpu.VMEM((2, SLOTS, T, 8, 128), BF16), pltpu.VMEM((2, SLOTS, T, 8, 128), BF16),
            pltpu.VMEM((2, 2, 4, T, 8, 128), F32), pltpu.VMEM((2, 2, 2, T, 8, 128), F32), pltpu.VMEM((2, 2, T, 8, 128), F32),
            pltpu.VMEM((2, SLOTS, T, 8, 128), BF16),
            dma(2, SLOTS), dma(5, 2, SLOTS), dma(5, 2, SLOTS), dma(2, SLOTS), dma(2, EACH), dma(2, EACH), dma(2), dma(2),
        ],
        compiler_params=pltpu.CompilerParams(collective_id=0, has_side_effects=True, vmem_limit_bytes=60 * 2**20),
    )(gg, gu, gd, md, vd)


def gathered(wg, wu, wd):
    shape = lambda s: jax.ShapeDtypeStruct(s, BF16)
    dma = lambda *s: pltpu.SemaphoreType.DMA(s)
    return pl.pallas_call(
        gather_kernel,
        name="gather",
        out_shape=[shape((2, 16, 2, TILES, 8, 128))] * 2 + [shape((2, 16, 2 * TILES, 8, 128))],
        in_specs=[pl.BlockSpec(memory_space=pltpu.VMEM)] * 3,
        out_specs=[pl.BlockSpec(memory_space=pl.ANY)] * 3,
        scratch_shapes=[dma(2, SLOTS), dma(5, 2, SLOTS), dma(5, 2, SLOTS)],
        compiler_params=pltpu.CompilerParams(collective_id=1, has_side_effects=True),
    )(wg, wu, wd)


def tiled(a):
    *lead, r, c = a.shape
    n = len(lead)
    a = a.reshape(*lead, r // 8, 8, c // 128, 128)
    return a.swapaxes(n + 1, n + 2).reshape(*lead, r // 8 * (c // 128), 8, 128)


def untiled(a, r, c):
    *lead, _, _, _ = a.shape
    n = len(lead)
    return a.reshape(*lead, r // 8, c // 128, 8, 128).swapaxes(n + 1, n + 2).reshape(*lead, r, c)


def adamw(w, m, v, g):
    m = 0.9 * m + 0.1 * g
    v = 0.95 * v + 0.05 * g * g
    step = m * lax.rsqrt(v + 1e-8) + 0.1 * w
    return (w - 0.02 * step).astype(jnp.bfloat16), m, v


def solution(mesh):
    def step(*arrays):
        terms, weights, m, v = (arrays[i : i + 3] for i in (0, 3, 6, 9))
        me = lax.axis_index("dp")
        chip, core = me // 2, me % 2
        gg, gu = (tiled(t[0]).reshape(2, 16, 2, TILES, 8, 128) for t in terms[:2])
        gd = tiled(terms[2][0]).reshape(2, 16, 2 * TILES, 8, 128)
        sg, su, sd, mp, vp = summed(gg, gu, gd, m[2], v[2])
        new = []
        for n, s in enumerate((sg, su)):
            w = lax.dynamic_slice_in_dim(weights[n], me * 48, 48, 1).astype(F32)
            new.append(adamw(w, m[n], v[n], untiled(s, 48, 4224).astype(F32)))
        sd = untiled(sd, 264, 1536)
        rows = sd.shape[1]
        wd = lax.dynamic_slice_in_dim(weights[2], chip * rows, rows, 1)
        half = rows // 2
        pick = lambda a: lax.dynamic_slice_in_dim(a, core * half, half, 1).astype(F32)
        _, md, vd = adamw(pick(wd), m[2], v[2], pick(sd))
        one = lambda a: lax.dynamic_index_in_dim(a, core, 0, False)
        both = lambda a, p: jnp.where(core == 0, jnp.concatenate([one(a), p]), jnp.concatenate([p, one(a)]))
        nd, _, _ = adamw(one(wd).astype(F32), both(m[2], mp), both(v[2], vp), one(sd).astype(F32))
        og, ou, od = gathered(tiled(new[0][0]), tiled(new[1][0]), tiled(nd))
        whole = [untiled(o.reshape(2, -1, 8, 128), r, c) for o, r, c in ((og, 1536, 4224), (ou, 1536, 4224), (od, 4224, 1536))]
        return (*whole, new[0][1], new[1][1], md, new[0][2], new[1][2], vd)

    all_of, cut = P(None, None, None), P(None, "dp", None)
    return jax.shard_map(
        step,
        mesh=mesh,
        in_specs=(P(("rep", "dp"), None, None, None),) * 3 + (all_of,) * 3 + (cut,) * 6,
        out_specs=(P("rep", None, None),) * 3 + (P("rep", "dp", None),) * 6,
        check_vma=False,
    )
```

time: 1550 us -> 676 us (0.44)
  waiting for transfers between devices: 1340 us -> 0 us
  Pallas kernels: 0 us -> 596 us
  local copies, waits for them, and re-layouts: 175 us -> 65.3 us
    pallas_call x0 -> x2, Pallas kernels: none -> 596 us  [the longest x1 300 us: gathered(): pl.pallas_call(gather_kernel, name='gather', out_shape=[shape((2, 16, 2,...]
    reduce_scatter x2 -> x0, waiting for transfers between devices: 492 us -> none  [step(): lax.psum_scatter(t[0], 'dp', scatter_dimension=1, tiled=True)]
    all_gather x3 -> x0, waiting for transfers between devices: 451 us -> none  [step(): whole = [lax.all_gather(one[0], 'dp', axis=1, tiled=True) for one in new]]
    unnamed x7 -> x0, waiting for transfers between devices: 402 us -> none
    unnamed x12 -> x37, local copies, waits for them, and re-layouts: 173 us -> 63.8 us
  transfers between devices with their start and end apart: 6 -> 0, of which waited for: 6 -> 0; matrix products, arithmetic and copies ran while one was open for 3% -> 0% of each run, Pallas kernels for 0% -> 0%
where the time goes in v1:
time: 676 us; the launch traced here: 675 us
  Pallas kernels  596 us (88%)
  local copies, waits for them, and re-layouts  65.3 us (10%)
  other arithmetic  13.6 us (2%)
    pallas_call x1, Pallas kernels, gathered(): pl.pallas_call(gather_kernel, name='gather', out_shape=[shape((2, 16, 2,...  300 us
    pallas_call x1, Pallas kernels, summed(): pl.pallas_call(sum_kernel, name='sums', out_shape=[shape((2, TILES, 8, 12...  295 us
    unnamed x37, local copies, waits for them, and re-layouts  63.8 us

profile of v1, /device:TPU:0, one launch (start us, length us, event | category | flops | bytes accessed | tf_op | source)
XLA Modules:
  0.0 675.3 jit_solution(14375433926279974858)
XLA Ops:
  0.7 0.0 copy-start.3
  0.7 1.9 copy.27.md
  2.5 0.0 copy-done.3
  2.6 0.0 copy-start
  2.6 0.3 copy.28.vd
  2.9 0.9 copy-done
  3.8 0.0 copy-start.1
  3.8 1.4 dynamic-slice_bitcast_fusion
  5.2 0.3 copy-done.1
  5.5 295.4 %sums.1 = (bf16[2,198,8,128]{3,2,1,0:T(8,128)(2,1)}, bf16[2,198,8,128]{3,2,1,0:T(8,128)(2,1)}, bf16[2,396,8,128]{3,2,1,0:T(8,128)(2,1)}, f32[132,1536]{1,0:T(8,128)}, f32[132,1536]{1,0:T(8,128)}) custom-call(bf16[2,16,2,198,8,128]{5,4,3,2,1,0:T(8,128)(2,1)} %bitcast.88, bf16[2,16,2,198,8,128]{5,4,3,2,1,0:T(8,128)(2,1)} %bitcast.89, ...), custom_call_target="tpu_custom_call" | custom-call | tf_op jit(solution)/shard_map/sums/pallas_call | solution.py:313
  300.9 0.0 copy-done.5
  300.9 0.0 copy-done.6
  300.9 0.0 copy-start.7
  300.9 4.0 fusion.10
  305.0 0.0 copy-done.7
  305.0 7.5 %fusion.4 = (bf16[2,48,4224]{2,1,0:T(8,128)(2,1)}, f32[2,48,4224]{2,1,0:T(8,128)}, f32[2,48,4224]{2,1,0:T(8,128)}, bf16[2,48,4224]{2,1,0:T(8,128)(2,1)}, f32[2,48,4224]{2,1,0:T(8,128)}, /*index=5*/f32[2,48,4224]{2,1,0:T(8,128)}) fusion(bf16[2,1536,4224]{2,1,0:T(8,128)(2,1)} %param.15, s32[]{:T(128)S(6)} %select_n.51, ...), kind=kLoop, calls=%fused_computation.17 | loop fusion | flops 12976128 | bytes 17842180 | tf_op jit(solution)/shard_map/convert_element_type | solution.py:361
  312.5 300.2 %gather.1 = (bf16[2,16,2,198,8,128]{5,4,3,2,1,0:T(8,128)(2,1)}, bf16[2,16,2,198,8,128]{5,4,3,2,1,0:T(8,128)(2,1)}, bf16[2,16,396,8,128]{4,3,2,1,0:T(8,128)(2,1)}) custom-call(bf16[2,198,8,128]{3,2,1,0:T(8,128)(2,1)} %bitcast.96, bf16[2,198,8,128]{3,2,1,0:T(8,128)(2,1)} %bitcast.97, bf16[396,8,128]{2,1,0:T(8,128)(2,1)} %bitcast.98), custom_call_target="tpu_custom_call" | custom-call | tf_op jit(solution)/shard_map/gather/pallas_call | solution.py:333
  612.7 0.0 copy-done.4
  612.7 0.0 copy-done.2
  612.7 2.1 fusion.1
  614.8 2.4 copy.33
  617.2 2.4 copy.34
  619.6 23.9 %copy.40 = bf16[2,1536,4224]{2,1,0:T(8,128)(2,1)} copy(bf16[2,1536,4224]{2,1,0:T(8,128)(2,1)} %bitcast.95) | data formatting | bytes 51904512
  643.5 22.6 %copy.41 = bf16[2,1536,4224]{2,1,0:T(8,128)(2,1)} copy(bf16[2,1536,4224]{2,1,0:T(8,128)(2,1)} %bitcast.94) | data formatting | bytes 51904512
  666.0 0.0 slice-done
  666.0 0.0 slice-done.1
  666.1 0.0 slice-done.2
  666.1 0.0 slice-done.3
  666.1 0.0 slice-done.4
  666.1 0.0 slice-done.5
  666.1 0.0 slice-done.6
  666.1 9.2 %copy.42 = bf16[2,4224,1536]{2,1,0:T(8,128)(2,1)} copy(bf16[2,4224,1536]{2,1,0:T(8,128)(2,1)S(1)} %bitcast.93) | data formatting | bytes 51904512
  (12 shorter events, 0.0 us)
Async XLA Ops:
  0.7 1.9 copy-start.3
  2.6 1.2 copy-start
  3.8 1.7 copy-start.1
  5.5 295.4 %copy-start.5 = (f32[132,1536]{1,0:T(8,128)S(1)}, f32[132,1536]{1,0:T(8,128)}, u32[]{:S(2)}) copy-start(f32[132,1536]{1,0:T(8,128)} %get-tuple-element.45) | copy-start | bytes 2433028
  5.5 295.4 %copy-start.6 = (f32[132,1536]{1,0:T(8,128)S(1)}, f32[132,1536]{1,0:T(8,128)}, u32[]{:S(2)}) copy-start(f32[132,1536]{1,0:T(8,128)} %get-tuple-element.46) | copy-start | bytes 2433028
  300.9 4.1 copy-start.7
  305.0 307.7 %copy-start.4 = (f32[2,132,1536]{2,0,1:T(2,128)S(1)}, f32[2,132,1536]{2,0,1:T(2,128)}, u32[]{:S(2)}) copy-start(f32[2,132,1536]{2,0,1:T(2,128)} %param.23) | copy-start | bytes 4866052
  312.5 300.2 %copy-start.2 = (f32[2,132,1536]{2,0,1:T(2,128)S(1)}, f32[2,132,1536]{2,0,1:T(2,128)}, u32[]{:S(2)}) copy-start(f32[2,132,1536]{2,0,1:T(2,128)} %param.20) | copy-start | bytes 4866052
  619.6 46.4 %slice-start = ((s8[25952256]{0:T(1024)(128)(4,1)}), s8[4194304]{0:T(1024)(128)(4,1)S(1)}, s32[]{:S(2)}) async-start(s8[25952256]{0:T(1024)(128)(4,1)} %bitcast.91), calls=%async_computation | async-start | bytes 8388608
  619.6 46.4 %slice-start.1 = ((s8[25952256]{0:T(1024)(128)(4,1)}), s8[4194304]{0:T(1024)(128)(4,1)S(1)}, s32[]{:S(2)}) async-start(s8[25952256]{0:T(1024)(128)(4,1)} %bitcast.91), calls=%async_computation.1 | async-start | bytes 8388608
  619.6 46.4 %slice-start.2 = ((s8[25952256]{0:T(1024)(128)(4,1)}), s8[4194304]{0:T(1024)(128)(4,1)S(1)}, s32[]{:S(2)}) async-start(s8[25952256]{0:T(1024)(128)(4,1)} %bitcast.91), calls=%async_computation.2 | async-start | bytes 8388608
  619.6 46.4 %slice-start.3 = ((s8[25952256]{0:T(1024)(128)(4,1)}), s8[4194304]{0:T(1024)(128)(4,1)S(1)}, s32[]{:S(2)}) async-start(s8[25952256]{0:T(1024)(128)(4,1)} %bitcast.91), calls=%async_computation.3 | async-start | bytes 8388608
  643.5 22.6 %slice-start.4 = ((s8[25952256]{0:T(1024)(128)(4,1)}), s8[4194304]{0:T(1024)(128)(4,1)S(1)}, s32[]{:S(2)}) async-start(s8[25952256]{0:T(1024)(128)(4,1)} %bitcast.91), calls=%async_computation.4 | async-start | bytes 8388608
  643.5 22.6 %slice-start.5 = ((s8[25952256]{0:T(1024)(128)(4,1)}), s8[4194304]{0:T(1024)(128)(4,1)S(1)}, s32[]{:S(2)}) async-start(s8[25952256]{0:T(1024)(128)(4,1)} %bitcast.91), calls=%async_computation.5 | async-start | bytes 8388608
  643.5 22.6 %slice-start.6 = ((s8[25952256]{0:T(1024)(128)(4,1)}), s8[786432]{0:T(1024)(128)(4,1)S(1)}, s32[]{:S(2)}) async-start(s8[25952256]{0:T(1024)(128)(4,1)} %bitcast.91), calls=%async_computation.6 | async-start | bytes 1572864

commit v2 on v0

v2 whole, which is shorter than its diff:
```python
import functools

import jax
import jax.numpy as jnp
from jax import lax
from jax.experimental import pallas as pl
from jax.experimental.pallas import tpu as pltpu
from jax.sharding import PartitionSpec as P

MESH = pl.DeviceIdType.MESH
F32, BF16 = jnp.float32, jnp.bfloat16
TILES = 198
T = 9
EACH = TILES // T
PAIRS = 3 * EACH
SLOTS = 4
LIVE = 5
X, Y = range(2)
WEIGHT = (8, 4)
ORDER = ((X, Y), (Y, X))
CORE, FIRST, IN, ACROSS, OUT, LAST, G_LAST, G_IN, G_ACROSS, G_OUT, G_FIRST, G_CORE = range(12)


class Place:
    def __init__(self):
        me = lax.axis_index("dp")
        self.core = lax.rem(me, 2)
        self.chip = lax.div(me, 2)
        self.z = z = lax.rem(self.chip, 4)
        self.bit = (lax.div(me, 16), lax.rem(lax.div(me, 8), 2))
        self.upper = lax.div(z, 2)
        self.lower = 1 - self.upper
        self.inner = lax.rem(z + self.upper, 2) == 1
        self.outer = lax.rem(z + self.upper, 2) == 0
        self.beside = z + 1 - 2 * lax.rem(z, 2)
        self.peer = me + 1 - 2 * self.core
        self.along = tuple(me + 2 * w * (1 - 2 * b) for w, b in zip(WEIGHT, self.bit))
        self.near = me + 2 * (self.beside - z)
        self.far = me + 2 * (3 - 2 * z)

    def greet(self):
        barrier = pltpu.get_barrier_semaphore()
        for other in (self.peer, *self.along, self.near, self.far):
            pl.semaphore_signal(barrier, inc=1, device_id={"dp": other}, device_id_type=MESH)
        pl.semaphore_wait(barrier, 5)


def for_chunk(i, colour, core, act):
    k = 2 * lax.rem(i, EACH) + colour
    for which in range(3):

        @pl.when(lax.div(i, EACH) == which)
        def _():
            if which < 2:
                act(which, lax.div(k, EACH), lax.rem(k, EACH) * T)
            else:
                act(which, core, k * T)


def kernel(
    gg, gu, gd, wg, wu, wd, mg, mu, md, vg, vu, vd, og, ou, od, ng, nu, nd, mx, vx,
    own, cor, s1, r1, s2, r2, s3, r3, s4, r4, s5, r5, acc, mv, wv, res, new,
    load_sem, ssem, rsem, out_sem, local_sem, par_sem, xs, xr, ms, mr,
):
    at = Place()
    core, bit, chip, z = at.core, at.bit, at.chip, at.z
    lower, upper = at.lower, at.upper
    at.greet()

    def send(stage, i, colour, src, dst, device):
        where = (stage, colour, lax.rem(i, SLOTS))
        return pltpu.make_async_remote_copy(
            src_ref=src, dst_ref=dst, send_sem=ssem.at[where], recv_sem=rsem.at[where], device_id={"dp": device}, device_id_type=MESH
        )

    def extra(src, dst, sems, where):
        return pltpu.make_async_remote_copy(
            src_ref=src, dst_ref=dst, send_sem=sems[0].at[where], recv_sem=sems[1].at[where], device_id={"dp": at.peer}, device_id_type=MESH
        )

    moments = [extra(src.at[1 - core], dst, (ms, mr), n) for n, (src, dst) in enumerate(((md, mx), (vd, vx)))]
    for copy in moments:
        copy.start()

    BUFFERS = {CORE: (own, cor), FIRST: (s1, r1), IN: (s2, r2), ACROSS: (s3, r3), OUT: (s4, r4), LAST: (s5, r5)}

    def device(stage, colour):
        b1, b3 = ORDER[colour]
        return {
            CORE: at.peer, FIRST: at.along[b1], IN: at.near, ACROSS: at.far, OUT: at.near, LAST: at.along[b3],
            G_LAST: at.along[b3], G_IN: at.near, G_ACROSS: at.far, G_OUT: at.near, G_FIRST: at.along[b1], G_CORE: at.peer,
        }[stage]

    BLOCKS = {G_LAST: 1, G_IN: 2, G_ACROSS: 4, G_OUT: 6, G_FIRST: 8, G_CORE: 16}

    def some(which, layer, first, q):
        return nd.at[layer, q, pl.ds(first, T)] if which == 2 else (ng, nu)[which].at[layer, q, core, pl.ds(first, T)]

    def whole(stage, i, colour):
        if stage in BUFFERS:
            src, dst = (ref.at[colour, lax.rem(i, SLOTS)] for ref in BUFFERS[stage])
        else:
            src = dst = some(0, 0, 0, pl.ds(0, BLOCKS[stage]))
        return send(stage, i, colour, src, dst, device(stage, colour))

    def free(stage, i, colour):
        pl.when(i >= SLOTS)(whole(stage, i, colour).wait_send)

    def load(i, colour, src):
        s = lax.rem(i, SLOTS)
        return pltpu.make_async_copy(src, own.at[colour, s], load_sem.at[colour, s])

    def fetch(i, colour):
        free(CORE, i, colour)

        def act(which, layer, first):
            if which < 2:
                g = (gg, gu)[which]
                a, b = (g.at[layer, :, c, pl.ds(first, T)] for c in (core, 1 - core))
            else:
                a, b = (gd.at[c, :, pl.ds(first, T)] for c in (core, 1 - core))
            send(CORE, i, colour, b, cor.at[colour, lax.rem(i, SLOTS)], at.peer).start()
            load(i, colour, a).start()

        for_chunk(i, colour, core, act)

    def number(colour, v1, v3, z):
        b1, b3 = ORDER[colour]
        return WEIGHT[b1] * v1 + WEIGHT[b3] * v3 + z

    def f32(ref):
        return ref[...].astype(F32)

    def loop(n, do):
        def one(j, _):
            do(j)
            return 0

        lax.fori_loop(0, n, one, 0)

    def sum_first(i, colour):
        s = lax.rem(i, SLOTS)
        load(i, colour, own.at[colour, s]).wait()
        whole(CORE, i, colour).wait_recv()
        free(FIRST, i, colour)

        def give(j):
            q = number(colour, 1 - bit[ORDER[colour][0]], lax.rem(j, 2), lax.div(j, 2))
            s1[colour, s, j] = (f32(own.at[colour, s, q]) + f32(cor.at[colour, s, q])).astype(BF16)

        loop(8, give)
        whole(FIRST, i, colour).start()

    def sum_in(i, colour):
        s = lax.rem(i, SLOTS)
        whole(FIRST, i, colour).wait_recv()

        def keep(j):
            q = number(colour, bit[ORDER[colour][0]], lax.rem(j, 2), lax.div(j, 2))
            acc[colour, lax.rem(i, LIVE), j] = f32(own.at[colour, s, q]) + f32(cor.at[colour, s, q]) + f32(r1.at[colour, s, j])

        loop(8, keep)

        @pl.when(at.outer)
        def _():
            free(IN, i, colour)

            def give(j):
                s2[colour, s, j] = acc[colour, lax.rem(i, LIVE), lower * 2 + j].astype(BF16)

            loop(6, give)
            whole(IN, i, colour).start()

    def sum_across(i, colour):
        s = lax.rem(i, SLOTS)

        @pl.when(at.inner)
        def _():
            whole(IN, i, colour).wait_recv()
            free(ACROSS, i, colour)

            def give(j):
                s3[colour, s, j] = (acc[colour, lax.rem(i, LIVE), lower * 4 + j] + f32(r2.at[colour, s, lower * 2 + j])).astype(BF16)

            loop(4, give)
            whole(ACROSS, i, colour).start()

            def keep(j):
                acc[colour, lax.rem(i, LIVE), z * 2 + j] += f32(r2.at[colour, s, (z - lower) * 2 + j])

            loop(2, keep)

    def sum_out(i, colour):
        s = lax.rem(i, SLOTS)

        @pl.when(at.inner)
        def _():
            whole(ACROSS, i, colour).wait_recv()
            free(OUT, i, colour)
            there = at.beside

            def give(j):
                s4[colour, s, j] = (acc[colour, lax.rem(i, LIVE), there * 2 + j] + f32(r3.at[colour, s, (there - 2 * upper) * 2 + j])).astype(BF16)

            loop(2, give)
            whole(OUT, i, colour).start()

            def keep(j):
                acc[colour, lax.rem(i, LIVE), z * 2 + j] += f32(r3.at[colour, s, (z - 2 * upper) * 2 + j])

            loop(2, keep)

    def params(i, colour, which, layer, first):
        two = lax.rem(i, 2)
        m, v, w = ((mg, vg, wg), (mu, vu, wu), (md, vd, wd))[which]
        here = pl.ds(first, T)
        pairs = [
            (m.at[layer, here], mv.at[colour, two, 0]),
            (v.at[layer, here], mv.at[colour, two, 1]),
            (w.at[layer, chip, here] if which == 2 else w.at[layer, chip, core, here], wv.at[colour, two]),
        ]
        if which == 2:
            pairs += [(mx.at[here], mv.at[colour, two, 2]), (vx.at[here], mv.at[colour, two, 3])]
        return [pltpu.make_async_copy(src, dst, par_sem.at[colour, two, n]) for n, (src, dst) in enumerate(pairs)]

    def sum_last(i, colour):
        s = lax.rem(i, SLOTS)

        if colour == 0:

            @pl.when(i == 2 * EACH)
            def _():
                for copy in moments:
                    copy.wait_recv()

        def act(*chunk):
            for copy in params(i, colour, *chunk):
                copy.start()

        for_chunk(i, colour, core, act)

        @pl.when(at.outer)
        def _():
            whole(OUT, i, colour).wait_recv()

            def keep(j):
                acc[colour, lax.rem(i, LIVE), z * 2 + j] += f32(r4.at[colour, s, j])

            loop(2, keep)

        free(LAST, i, colour)
        s5[colour, s] = acc[colour, lax.rem(i, LIVE), z * 2 + 1 - bit[ORDER[colour][1]]].astype(BF16)
        whole(LAST, i, colour).start()

    def result(i, colour, which, layer, first):
        s = lax.rem(i, SLOTS)
        return pltpu.make_async_copy(res.at[colour, s], (og, ou, od)[which].at[layer, pl.ds(first, T)], out_sem.at[colour, s])

    def share(i, colour, first):
        return extra(res.at[colour, lax.rem(i, SLOTS)], od.at[core, pl.ds(first, T)], (xs, xr), (colour, i - 2 * EACH))

    def local(i, colour, which, layer, first):
        s = lax.rem(i, SLOTS)
        return pltpu.make_async_copy(new.at[colour, s], some(which, layer, first, chip), local_sem.at[colour, s])

    def update(i, colour):
        s, two = lax.rem(i, SLOTS), lax.rem(i, 2)
        whole(LAST, i, colour).wait_recv()
        pl.when(i >= SLOTS)(result(i, colour, 0, 0, 0).wait)
        pl.when(i >= SLOTS + 2 * EACH)(share(i - SLOTS, colour, 0).wait_send)
        res[colour, s] = (acc[colour, lax.rem(i, LIVE), z * 2 + bit[ORDER[colour][1]]] + f32(r5.at[colour, s])).astype(BF16)
        for copy in params(i, colour, 0, 0, 0):
            copy.wait()

        @pl.when(i >= 2 * EACH)
        def _():
            for copy in params(i, colour, 2, 0, 0)[3:]:
                copy.wait()
            for n in range(2):
                mv[colour, two, n] += mv[colour, two, 2 + n]

        free(G_LAST, i, colour)
        new[colour, s] = adamw(f32(wv.at[colour, two]), mv[colour, two, 0], mv[colour, two, 1], f32(res.at[colour, s]))[0]

        def act(which, layer, first):
            send(G_LAST, i, colour, new.at[colour, s], some(which, layer, first, chip), device(G_LAST, colour)).start()
            local(i, colour, which, layer, first).start()
            result(i, colour, which, layer, first).start()
            if which == 2:
                share(i, colour, first).start()

        for_chunk(i, colour, core, act)

    def units(stage, i, colour, zs):
        free(stage, i, colour)
        v1 = bit[ORDER[colour][0]]

        def act(which, layer, first):
            for there in zs:
                for v3 in range(2):
                    part = some(which, layer, first, number(colour, v1, v3, there))
                    send(stage, i, colour, part, part, device(stage, colour)).start()

        for_chunk(i, colour, core, act)

    def gather_in(i, colour):
        local(i, colour, 0, 0, 0).wait()
        whole(G_LAST, i, colour).wait_recv()
        pl.when(at.outer)(lambda: units(G_IN, i, colour, (z,)))

    def gather_across(i, colour):
        @pl.when(at.inner)
        def _():
            whole(G_IN, i, colour).wait_recv()
            units(G_ACROSS, i, colour, (z, at.beside))

    def gather_out(i, colour):
        @pl.when(at.inner)
        def _():
            whole(G_ACROSS, i, colour).wait_recv()
            units(G_OUT, i, colour, (z, 3 - z, 3 - at.beside))

    def gather_first(i, colour):
        pl.when(at.outer)(whole(G_OUT, i, colour).wait_recv)
        free(G_FIRST, i, colour)

        def act(which, layer, first):
            if ORDER[colour][0] == X:
                parts = [pl.ds(8 * bit[X], 8)]
            else:
                parts = [pl.ds(4 * bit[Y] + 8 * n, 4) for n in range(2)]
            for q in parts:
                part = some(which, layer, first, q)
                send(G_FIRST, i, colour, part, part, device(G_FIRST, colour)).start()

        for_chunk(i, colour, core, act)

    def gather_core(i, colour):
        whole(G_FIRST, i, colour).wait_recv()
        free(G_CORE, i, colour)

        def act(which, layer, first):
            part = some(which, layer, first, slice(None))
            send(G_CORE, i, colour, part, part, at.peer).start()

        for_chunk(i, colour, core, act)

    def gather_done(i, colour):
        whole(G_CORE, i, colour).wait_recv()

    for colour in range(2):
        fetch(0, colour)

    stages = (
        sum_first, None, sum_in, sum_across, sum_out, sum_last, update,
        gather_in, gather_across, gather_out, gather_first, gather_core, gather_done,
    )

    def step(i, _):
        late = 0
        for stage in stages:
            if stage is None:

                @pl.when(i + 1 < PAIRS)
                def _():
                    for colour in range(2):
                        fetch(i + 1, colour)

                continue

            @pl.when((i >= late) & (i < PAIRS + late))
            def _():
                for colour in range(2):
                    stage(i - late, colour)

            late += 1
        return 0

    lax.fori_loop(0, PAIRS + len(stages) - 2, step, 0)
    for colour in range(2):
        for i in range(PAIRS - SLOTS, PAIRS):
            for stage in (CORE, FIRST, LAST, G_LAST, G_FIRST, G_CORE):
                whole(stage, i, colour).wait_send()

            @pl.when(at.outer)
            def _():
                for stage in (IN, G_IN):
                    whole(stage, i, colour).wait_send()

            @pl.when(at.inner)
            def _():
                for stage in (ACROSS, OUT, G_ACROSS, G_OUT):
                    whole(stage, i, colour).wait_send()

            result(i, colour, 0, 0, 0).wait()
            share(i, colour, 0).wait_send()
        for i in range(2 * EACH, PAIRS):
            share(i, colour, 0).wait_recv()
    for copy in moments:
        copy.wait_send()


def fused(*arrays):
    any_ = pl.BlockSpec(memory_space=pl.ANY)
    shape = lambda s, d=BF16: jax.ShapeDtypeStruct(s, d)
    vmem = lambda *n, k=SLOTS, d=BF16: pltpu.VMEM((2, k, *n, T, 8, 128), d)
    dma = lambda *s: pltpu.SemaphoreType.DMA(s)
    sums = [shape((2, n * TILES, 8, 128)) for n in (1, 1, 2)]
    wholes = [shape((2, 16, 2, TILES, 8, 128))] * 2 + [shape((2, 16, 2 * TILES, 8, 128))]
    return pl.pallas_call(
        kernel,
        name="fused",
        out_shape=sums + wholes + [shape((2 * TILES, 8, 128), F32)] * 2,
        in_specs=[any_] * 12,
        out_specs=[any_] * 8,
        scratch_shapes=[
            *(vmem(n) for n in (16, 16, 8, 8, 6, 6, 4, 4, 2, 2)), vmem(), vmem(),
            vmem(8, k=LIVE, d=F32), vmem(4, k=2, d=F32), vmem(k=2), vmem(), vmem(),
            dma(2, SLOTS), dma(12, 2, SLOTS), dma(12, 2, SLOTS), dma(2, SLOTS), dma(2, SLOTS), dma(2, 2, 5),
            dma(2, EACH), dma(2, EACH), dma(2), dma(2),
        ],
        compiler_params=pltpu.CompilerParams(collective_id=0, has_side_effects=True, vmem_limit_bytes=60 * 2**20),
    )(*arrays)


def tiled(a):
    *lead, r, c = a.shape
    n = len(lead)
    a = a.reshape(*lead, r // 8, 8, c // 128, 128)
    return a.swapaxes(n + 1, n + 2).reshape(*lead, r // 8 * (c // 128), 8, 128)


def untiled(a, r, c):
    *lead, _, _, _ = a.shape
    n = len(lead)
    return a.reshape(*lead, r // 8, c // 128, 8, 128).swapaxes(n + 1, n + 2).reshape(*lead, r, c)


def adamw(w, m, v, g):
    m = 0.9 * m + 0.1 * g
    v = 0.95 * v + 0.05 * g * g
    step = m * lax.rsqrt(v + 1e-8) + 0.1 * w
    return (w - 0.02 * step).astype(jnp.bfloat16), m, v


def solution(mesh):
    def step(*arrays):
        terms, weights, m, v = (arrays[i : i + 3] for i in (0, 3, 6, 9))
        core = lax.axis_index("dp") % 2
        half = m[2].shape[1]
        six = lambda a: tiled(a).reshape(2, 16, 2, TILES, 8, 128)
        five = lambda a: tiled(a).reshape(2, 16, 2 * TILES, 8, 128)
        placed = lambda a: tiled(lax.dynamic_update_slice_in_dim(jnp.zeros((2, 2 * half, 1536), F32), a, core * half, 1))
        sg, su, sd, og, ou, od, _, _ = fused(
            six(terms[0][0]), six(terms[1][0]), five(terms[2][0]), six(weights[0]), six(weights[1]), five(weights[2]),
            tiled(m[0]), tiled(m[1]), placed(m[2]), tiled(v[0]), tiled(v[1]), placed(v[2]),
        )
        sd = lax.dynamic_slice_in_dim(untiled(sd, 2 * half, 1536), core * half, half, 1)
        new = []
        for n, g in enumerate((untiled(sg, 48, 4224), untiled(su, 48, 4224), sd)):
            new.append(adamw(jnp.zeros((), F32), m[n], v[n], g.astype(F32))[1:])
        whole = [untiled(o.reshape(2, -1, 8, 128), r, c) for o, r, c in ((og, 1536, 4224), (ou, 1536, 4224), (od, 4224, 1536))]
        return (*whole, *(one[0] for one in new), *(one[1] for one in new))

    all_of, cut = P(None, None, None), P(None, "dp", None)
    return jax.shard_map(
        step,
        mesh=mesh,
        in_specs=(P(("rep", "dp"), None, None, None),) * 3 + (all_of,) * 3 + (cut,) * 6,
        out_specs=(P("rep", None, None),) * 3 + (P("rep", "dp", None),) * 6,
        check_vma=False,
    )
```

time: 1550 us -> 594 us (0.38)
  waiting for transfers between devices: 1340 us -> 0 us
  Pallas kernels: 0 us -> 514 us
  local copies, waits for them, and re-layouts: 175 us -> 67.9 us
    pallas_call x0 -> x1, Pallas kernels: none -> 514 us  [fused(): pl.pallas_call(kernel, name='fused', out_shape=sums + wholes + [shape((2...]
    reduce_scatter x2 -> x0, waiting for transfers between devices: 492 us -> none  [step(): lax.psum_scatter(t[0], 'dp', scatter_dimension=1, tiled=True)]
    all_gather x3 -> x0, waiting for transfers between devices: 451 us -> none  [step(): whole = [lax.all_gather(one[0], 'dp', axis=1, tiled=True) for one in new]]
    unnamed x7 -> x0, waiting for transfers between devices: 402 us -> none
    unnamed x12 -> x27, local copies, waits for them, and re-layouts: 173 us -> 59.9 us
    convert_element_type x3 -> x0, other arithmetic: 16.2 us -> none  [adamw(): return ((w - 0.02 * step).astype(jnp.bfloat16), m, v)]
  transfers between devices with their start and end apart: 6 -> 0, of which waited for: 6 -> 0; matrix products, arithmetic and copies ran while one was open for 3% -> 0% of each run, Pallas kernels for 0% -> 0%
where the time goes in v2:
time: 594 us
  Pallas kernels  514 us (87%)
  local copies, waits for them, and re-layouts  67.9 us (11%)
  other arithmetic  10.8 us (2%)
    pallas_call x1, Pallas kernels, fused(): pl.pallas_call(kernel, name='fused', out_shape=sums + wholes + [shape((2...  514 us
    unnamed x27, local copies, waits for them, and re-layouts  59.9 us

profile of v2, /device:TPU:0, one launch (start us, length us, event | category | flops | bytes accessed | tf_op | source)
XLA Modules:
  0.0 593.6 jit_solution(2737485623794687924)
XLA Ops:
  0.6 2.9 copy.22
  3.6 0.4 broadcast.16.clone
  3.9 3.6 dynamic_update_slice.6
  7.6 0.0 copy-start.2
  7.6 1.7 copy-done.2
  9.3 2.9 copy.23
  12.2 0.4 broadcast.16.clone.1
  12.6 3.6 dynamic_update_slice.7
  16.2 0.0 copy-start.1
  16.2 1.7 copy-done.1
  17.9 514.1 %fused.1 = (bf16[2,198,8,128]{3,2,1,0:T(8,128)(2,1)}, bf16[2,198,8,128]{3,2,1,0:T(8,128)(2,1)}, bf16[2,396,8,128]{3,2,1,0:T(8,128)(2,1)}, bf16[2,16,2,198,8,128]...) custom-call(bf16[2,16,2,198,8,128]{5,4,3,2,1,0:T(8,128)(2,1)} %bitca, ...), custom_call_target="tpu_custom_call" | custom-call | tf_op jit(solution)/shard_map/fused/pallas_call | solution.py:410
  532.0 0.0 copy-start
  532.0 7.0 %fusion.2 = (f32[2,48,4224]{2,1,0:T(8,128)}, f32[2,48,4224]{2,1,0:T(8,128)}, f32[2,48,4224]{2,1,0:T(8,128)}, f32[2,48,4224]{2,1,0:T(8,128)}) fusion(bf16[2,6,33,8,128]{4,3,2,1,0:T(8,128)(2,1)} %bitcast.115, f32[2,48,4224]{2,1,0:T(8,128)} %param.21, f32[2,48,4224]{2,1,0:T(8,128)} %param.18, bf16[2,6,33,8,128]{4,3,2,1,0:T(8,128)(2,1)} %bitcast.116, ...), kind=kLoop, calls=%fused_computation.6 | loop fusion | flops 6488064 | bytes 14598144 | tf_op jit(solution)/shard_map/add | solution.py:441
  539.0 3.8 fusion.1
  542.8 2.4 copy.26
  545.3 2.4 copy.27
  547.7 0.0 copy-done
  547.7 0.0 slice-start
  547.7 0.0 slice-start.1
  547.7 0.0 slice-start.2
  547.7 0.0 slice-start.3
  547.7 13.1 %copy.35 = bf16[2,1536,4224]{2,1,0:T(8,128)(2,1)} copy(bf16[2,1536,4224]{2,1,0:T(8,128)(2,1)S(1)} %bitcast.102) | data formatting | bytes 51904512
  560.8 0.0 slice-start.4
  560.8 23.5 %copy.36 = bf16[2,1536,4224]{2,1,0:T(8,128)(2,1)} copy(bf16[2,1536,4224]{2,1,0:T(8,128)(2,1)} %bitcast.101) | data formatting | bytes 51904512
  584.4 0.0 slice-done
  584.4 0.0 slice-done.1
  584.4 0.0 slice-done.2
  584.4 0.0 slice-done.3
  584.4 0.0 slice-done.4
  584.4 0.0 slice-done.5
  584.4 0.0 slice-done.6
  584.4 9.2 %copy.37 = bf16[2,4224,1536]{2,1,0:T(8,128)(2,1)} copy(bf16[2,4224,1536]{2,1,0:T(8,128)(2,1)S(1)} %bitcast.100) | data formatting | bytes 51904512
  (3 shorter events, 0.0 us)
Async XLA Ops:
  7.6 1.7 copy-start.2
  16.2 1.7 copy-start.1
  532.0 15.7 %copy-start = (bf16[2,16,2,198,8,128]{5,4,3,2,1,0:T(8,128)(2,1)S(1)}, bf16[2,16,2,198,8,128]{5,4,3,2,1,0:T(8,128)(2,1)}, u32[]{:S(2)}) copy-start(bf16[2,16,2,198,8,128]{5,4,3,2,1,0:T(8,128)(2,1)} %get-tuple-element.15) | copy-start | bytes 77856768
  547.7 36.7 %slice-start = ((s8[25952256]{0:T(1024)(128)(4,1)}), s8[4194304]{0:T(1024)(128)(4,1)S(1)}, s32[]{:S(2)}) async-start(s8[25952256]{0:T(1024)(128)(4,1)} %bitcast.98), calls=%async_computation | async-start | bytes 8388608
  547.7 36.7 %slice-start.1 = ((s8[25952256]{0:T(1024)(128)(4,1)}), s8[4194304]{0:T(1024)(128)(4,1)S(1)}, s32[]{:S(2)}) async-start(s8[25952256]{0:T(1024)(128)(4,1)} %bitcast.98), calls=%async_computation.1 | async-start | bytes 8388608
  547.7 36.7 %slice-start.2 = ((s8[25952256]{0:T(1024)(128)(4,1)}), s8[4194304]{0:T(1024)(128)(4,1)S(1)}, s32[]{:S(2)}) async-start(s8[25952256]{0:T(1024)(128)(4,1)} %bitcast.98), calls=%async_computation.2 | async-start | bytes 8388608
  547.7 36.7 %slice-start.3 = ((s8[25952256]{0:T(1024)(128)(4,1)}), s8[4194304]{0:T(1024)(128)(4,1)S(1)}, s32[]{:S(2)}) async-start(s8[25952256]{0:T(1024)(128)(4,1)} %bitcast.98), calls=%async_computation.3 | async-start | bytes 8388608
  560.8 23.6 %slice-start.4 = ((s8[25952256]{0:T(1024)(128)(4,1)}), s8[4194304]{0:T(1024)(128)(4,1)S(1)}, s32[]{:S(2)}) async-start(s8[25952256]{0:T(1024)(128)(4,1)} %bitcast.98), calls=%async_computation.4 | async-start | bytes 8388608
  560.8 23.6 %slice-start.5 = ((s8[25952256]{0:T(1024)(128)(4,1)}), s8[4194304]{0:T(1024)(128)(4,1)S(1)}, s32[]{:S(2)}) async-start(s8[25952256]{0:T(1024)(128)(4,1)} %bitcast.98), calls=%async_computation.5 | async-start | bytes 8388608
  560.8 23.6 %slice-start.6 = ((s8[25952256]{0:T(1024)(128)(4,1)}), s8[786432]{0:T(1024)(128)(4,1)S(1)}, s32[]{:S(2)}) async-start(s8[25952256]{0:T(1024)(128)(4,1)} %bitcast.98), calls=%async_computation.6 | async-start | bytes 1572864

commit v3 on v2

--- a/solution.py
+++ b/solution.py
@@ -10,7 +10,7 @@
 MESH = pl.DeviceIdType.MESH
 F32, BF16 = jnp.float32, jnp.bfloat16
 TILES = 198
-T = 9
+T = 6
 EACH = TILES // T
 PAIRS = 3 * EACH
 SLOTS = 4
@@ -450,7 +450,8 @@
         half = m[2].shape[1]
         six = lambda a: tiled(a).reshape(2, 16, 2, TILES, 8, 128)
         five = lambda a: tiled(a).reshape(2, 16, 2 * TILES, 8, 128)
-        placed = lambda a: tiled(lax.dynamic_update_slice_in_dim(jnp.zeros((2, 2 * half, 1536), F32), a, core * half, 1))
+        side = lambda a, lo: lax.pad(a, jnp.zeros((), F32), ((0, 0, 0), (lo, half - lo, 0), (0, 0, 0)))
+        placed = lambda a: tiled(jnp.where(core == 0, side(a, 0), side(a, half)))
         sg, su, sd, og, ou, od, _, _ = fused(
             six(terms[0][0]), six(terms[1][0]), five(terms[2][0]), six(weights[0]), six(weights[1]), five(weights[2]),
             tiled(m[0]), tiled(m[1]), placed(m[2]), tiled(v[0]), tiled(v[1]), placed(v[2]),

time: 594 us -> 579 us (0.975)
  local copies, waits for them, and re-layouts: 67.9 us -> 52.9 us
    dynamic_update_slice x2 -> x0, local copies, waits for them, and re-layouts: 7.24 us -> none  [step(): lax.dynamic_update_slice_in_dim(jnp.zeros((2, 2 * half, 1536), F32), a, c...]
    unnamed x27 -> x25, local copies, waits for them, and re-layouts: 59.9 us -> 52.9 us
    add x2 -> x3, other arithmetic: 10.8 us -> 12.6 us  [adamw(): v = 0.95 * v + 0.05 * g * g]
where the time goes in v3:
time: 579 us
  Pallas kernels  509 us (88%)
  local copies, waits for them, and re-layouts  52.9 us (9%)
  other arithmetic  16.2 us (3%)
    pallas_call x1, Pallas kernels, fused(): pl.pallas_call(kernel, name='fused', out_shape=sums + wholes + [shape((2...  509 us
    unnamed x25, local copies, waits for them, and re-layouts  52.9 us
    add x3, other arithmetic, adamw(): v = 0.95 * v + 0.05 * g * g  12.6 us

profile of v3, /device:TPU:0, one launch (start us, length us, event | category | flops | bytes accessed | tf_op | source)
XLA Modules:
  0.0 578.7 jit_solution(11074411578075386085)
XLA Ops:
  0.7 0.0 copy-start.1
  0.7 1.9 copy.24
  2.5 0.0 copy-done.1
  2.6 0.3 copy.26
  2.9 3.7 pad_select_fusion
  6.6 508.8 %fused.1 = (bf16[2,198,8,128]{3,2,1,0:T(8,128)(2,1)}, bf16[2,198,8,128]{3,2,1,0:T(8,128)(2,1)}, bf16[2,396,8,128]{3,2,1,0:T(8,128)(2,1)}, bf16[2,16,2,198,8,128]...) custom-call(bf16[2,16,2,198,8,128]{5,4,3,2,1,0:T(8,128)(2,1)} %bitca, ...), custom_call_target="tpu_custom_call" | custom-call | tf_op jit(solution)/shard_map/fused/pallas_call | solution.py:410
  515.4 0.0 copy-start
  515.4 3.2 fusion.1
  518.6 2.4 copy.30
  521.0 2.4 copy.31
  523.4 5.0 fusion.2
  528.5 4.3 fusion.3
  532.8 0.0 copy-done
  532.8 0.0 slice-start
  532.8 0.0 slice-start.1
  532.8 0.0 slice-start.2
  532.8 0.0 slice-start.3
  532.8 13.1 %copy.37 = bf16[2,1536,4224]{2,1,0:T(8,128)(2,1)} copy(bf16[2,1536,4224]{2,1,0:T(8,128)(2,1)S(1)} %bitcast.102) | data formatting | bytes 51904512
  545.9 0.0 slice-start.4
  545.9 0.0 slice-start.5
  545.9 0.0 slice-start.6
  545.9 23.5 %copy.38 = bf16[2,1536,4224]{2,1,0:T(8,128)(2,1)} copy(bf16[2,1536,4224]{2,1,0:T(8,128)(2,1)} %bitcast.101) | data formatting | bytes 51904512
  569.5 0.0 slice-done
  569.5 0.0 slice-done.1
  569.5 0.0 slice-done.2
  569.5 0.0 slice-done.3
  569.5 0.0 slice-done.4
  569.5 0.0 slice-done.5
  569.5 0.0 slice-done.6
  569.5 9.2 %copy.39 = bf16[2,4224,1536]{2,1,0:T(8,128)(2,1)} copy(bf16[2,4224,1536]{2,1,0:T(8,128)(2,1)S(1)} %bitcast.100) | data formatting | bytes 51904512
  (1 shorter events, 0.0 us)
Async XLA Ops:
  0.7 1.9 copy-start.1
  515.4 17.4 %copy-start = (bf16[2,16,2,198,8,128]{5,4,3,2,1,0:T(8,128)(2,1)S(1)}, bf16[2,16,2,198,8,128]{5,4,3,2,1,0:T(8,128)(2,1)}, u32[]{:S(2)}) copy-start(bf16[2,16,2,198,8,128]{5,4,3,2,1,0:T(8,128)(2,1)} %get-tuple-element.15) | copy-start | bytes 77856768
  532.8 36.7 %slice-start = ((s8[25952256]{0:T(1024)(128)(4,1)}), s8[4194304]{0:T(1024)(128)(4,1)S(1)}, s32[]{:S(2)}) async-start(s8[25952256]{0:T(1024)(128)(4,1)} %bitcast.98), calls=%async_computation | async-start | bytes 8388608
  532.8 36.7 %slice-start.1 = ((s8[25952256]{0:T(1024)(128)(4,1)}), s8[4194304]{0:T(1024)(128)(4,1)S(1)}, s32[]{:S(2)}) async-start(s8[25952256]{0:T(1024)(128)(4,1)} %bitcast.98), calls=%async_computation.1 | async-start | bytes 8388608
  532.8 36.7 %slice-start.2 = ((s8[25952256]{0:T(1024)(128)(4,1)}), s8[4194304]{0:T(1024)(128)(4,1)S(1)}, s32[]{:S(2)}) async-start(s8[25952256]{0:T(1024)(128)(4,1)} %bitcast.98), calls=%async_computation.2 | async-start | bytes 8388608
  532.8 36.7 %slice-start.3 = ((s8[25952256]{0:T(1024)(128)(4,1)}), s8[4194304]{0:T(1024)(128)(4,1)S(1)}, s32[]{:S(2)}) async-start(s8[25952256]{0:T(1024)(128)(4,1)} %bitcast.98), calls=%async_computation.3 | async-start | bytes 8388608
  545.9 23.6 %slice-start.4 = ((s8[25952256]{0:T(1024)(128)(4,1)}), s8[4194304]{0:T(1024)(128)(4,1)S(1)}, s32[]{:S(2)}) async-start(s8[25952256]{0:T(1024)(128)(4,1)} %bitcast.98), calls=%async_computation.4 | async-start | bytes 8388608
  545.9 23.6 %slice-start.5 = ((s8[25952256]{0:T(1024)(128)(4,1)}), s8[4194304]{0:T(1024)(128)(4,1)S(1)}, s32[]{:S(2)}) async-start(s8[25952256]{0:T(1024)(128)(4,1)} %bitcast.98), calls=%async_computation.5 | async-start | bytes 8388608
  545.9 23.6 %slice-start.6 = ((s8[25952256]{0:T(1024)(128)(4,1)}), s8[786432]{0:T(1024)(128)(4,1)S(1)}, s32[]{:S(2)}) async-start(s8[25952256]{0:T(1024)(128)(4,1)} %bitcast.98), calls=%async_computation.6 | async-start | bytes 1572864

commit v4 on v3

--- a/solution.py
+++ b/solution.py
@@ -14,6 +14,7 @@
 EACH = TILES // T
 PAIRS = 3 * EACH
 SLOTS = 4
+HELD, EDGE = 204, 192
 LIVE = 5
 X, Y = range(2)
 WEIGHT = (8, 4)
@@ -212,16 +213,25 @@
 
     def params(i, colour, which, layer, first):
         two = lax.rem(i, 2)
-        m, v, w = ((mg, vg, wg), (mu, vu, wu), (md, vd, wd))[which]
         here = pl.ds(first, T)
-        pairs = [
-            (m.at[layer, here], mv.at[colour, two, 0]),
-            (v.at[layer, here], mv.at[colour, two, 1]),
-            (w.at[layer, chip, here] if which == 2 else w.at[layer, chip, core, here], wv.at[colour, two]),
-        ]
-        if which == 2:
-            pairs += [(mx.at[here], mv.at[colour, two, 2]), (vx.at[here], mv.at[colour, two, 3])]
-        return [pltpu.make_async_copy(src, dst, par_sem.at[colour, two, n]) for n, (src, dst) in enumerate(pairs)]
+
+        def copies(*pairs):
+            return [pltpu.make_async_copy(src, dst, par_sem.at[colour, two, n]) for n, src, dst in pairs]
+
+        def both(m, v, n, sem):
+            return copies((sem, m, mv.at[colour, two, n]), (sem + 1, v, mv.at[colour, two, n + 1]))
+
+        w = (wg, wu, wd)[which]
+        weight = copies((2, w.at[layer, chip, here] if which == 2 else w.at[layer, chip, core, here], wv.at[colour, two]))
+        if which < 2:
+            m, v = ((mg, vg), (mu, vu))[which]
+            return weight + both(m.at[layer, here], v.at[layer, here], 0, 0), [], []
+        ours, theirs = pl.ds(first - EDGE * core, T), pl.ds(first - EDGE * (1 - core), T)
+        return (
+            weight + both(md.at[core, ours], vd.at[core, ours], 0, 0),
+            both(mx.at[theirs], vx.at[theirs], 0, 0),
+            both(mx.at[theirs], vx.at[theirs], 2, 3),
+        )
 
     def sum_last(i, colour):
         s = lax.rem(i, SLOTS)
@@ -234,8 +244,20 @@
                     copy.wait_recv()
 
         def act(*chunk):
-            for copy in params(i, colour, *chunk):
-                copy.start()
+            here, there, edge = params(i, colour, *chunk)
+            if not edge:
+                for copy in here:
+                    copy.start()
+                return
+            first = chunk[2]
+            here[0].start()
+            mine = ((core == 0) & (first < HELD)) | ((core == 1) & (first >= EDGE))
+            for condition, some_ in ((mine, here[1:]), (~mine, there), ((first >= EDGE) & (first < HELD), edge)):
+
+                @pl.when(condition)
+                def _():
+                    for copy in some_:
+                        copy.start()
 
         for_chunk(i, colour, core, act)
 
@@ -269,13 +291,14 @@
         pl.when(i >= SLOTS)(result(i, colour, 0, 0, 0).wait)
         pl.when(i >= SLOTS + 2 * EACH)(share(i - SLOTS, colour, 0).wait_send)
         res[colour, s] = (acc[colour, lax.rem(i, LIVE), z * 2 + bit[ORDER[colour][1]]] + f32(r5.at[colour, s])).astype(BF16)
-        for copy in params(i, colour, 0, 0, 0):
+        for copy in params(i, colour, 0, 0, 0)[0]:
             copy.wait()
-
-        @pl.when(i >= 2 * EACH)
-        def _():
-            for copy in params(i, colour, 2, 0, 0)[3:]:
-                copy.wait()
+        first = (2 * lax.rem(i, EACH) + colour) * T
+
+        @pl.when((i >= 2 * EACH) & (first >= EDGE) & (first < HELD))
+        def _():
+            for n in range(2):
+                pltpu.make_async_copy(mv.at[colour, two, n], mv.at[colour, two, 2 + n], par_sem.at[colour, two, 3 + n]).wait()
             for n in range(2):
                 mv[colour, two, n] += mv[colour, two, 2 + n]
 
@@ -410,7 +433,7 @@
     return pl.pallas_call(
         kernel,
         name="fused",
-        out_shape=sums + wholes + [shape((2 * TILES, 8, 128), F32)] * 2,
+        out_shape=sums + wholes + [shape((HELD, 8, 128), F32)] * 2,
         in_specs=[any_] * 12,
         out_specs=[any_] * 8,
         scratch_shapes=[
@@ -450,8 +473,8 @@
         half = m[2].shape[1]
         six = lambda a: tiled(a).reshape(2, 16, 2, TILES, 8, 128)
         five = lambda a: tiled(a).reshape(2, 16, 2 * TILES, 8, 128)
-        side = lambda a, lo: lax.pad(a, jnp.zeros((), F32), ((0, 0, 0), (lo, half - lo, 0), (0, 0, 0)))
-        placed = lambda a: tiled(jnp.where(core == 0, side(a, 0), side(a, half)))
+        side = lambda a, lo: lax.pad(a, jnp.zeros((), F32), ((0, 0, 0), (lo, -half % 8 - lo, 0), (0, 0, 0)))
+        placed = lambda a: tiled(jnp.where(core == 0, side(a, 0), side(a, -half % 8)))
         sg, su, sd, og, ou, od, _, _ = fused(
             six(terms[0][0]), six(terms[1][0]), five(terms[2][0]), six(weights[0]), six(weights[1]), five(weights[2]),
             tiled(m[0]), tiled(m[1]), placed(m[2]), tiled(v[0]), tiled(v[1]), placed(v[2]),

time: 579 us -> 575 us (level)
  no operation moved by 1% of the time
where the time goes in v4:
time: 575 us
  Pallas kernels  507 us (88%)
  local copies, waits for them, and re-layouts  52.9 us (9%)
  other arithmetic  14.8 us (3%)
    pallas_call x1, Pallas kernels, fused(): pl.pallas_call(kernel, name='fused', out_shape=sums + wholes + [shape((HE...  507 us
    unnamed x25, local copies, waits for them, and re-layouts  52.9 us
    add x3, other arithmetic, adamw(): v = 0.95 * v + 0.05 * g * g  12.6 us

profile of v4, /device:TPU:0, one launch (start us, length us, event | category | flops | bytes accessed | tf_op | source)
XLA Modules:
  0.0 575.0 jit_solution(13360099125567076430)
XLA Ops:
  0.7 0.0 copy-start.1
  0.7 1.9 copy.24
  2.5 0.0 copy-done.1
  2.6 0.3 copy.26
  2.9 2.2 pad_select_fusion
  5.1 506.6 %fused.1 = (bf16[2,198,8,128]{3,2,1,0:T(8,128)(2,1)}, bf16[2,198,8,128]{3,2,1,0:T(8,128)(2,1)}, bf16[2,396,8,128]{3,2,1,0:T(8,128)(2,1)}, bf16[2,16,2,198,8,128]...) custom-call(bf16[2,16,2,198,8,128]{5,4,3,2,1,0:T(8,128)(2,1)} %bitca, ...), custom_call_target="tpu_custom_call" | custom-call | tf_op jit(solution)/shard_map/fused/pallas_call | solution.py:433
  511.6 0.0 copy-start
  511.7 3.2 fusion.1
  514.9 2.4 copy.30
  517.3 2.4 copy.31
  519.7 5.0 fusion.2
  524.8 4.3 fusion.3
  529.0 0.0 copy-done
  529.0 0.0 slice-start
  529.0 0.0 slice-start.1
  529.1 0.0 slice-start.2
  529.1 0.0 slice-start.3
  529.1 13.1 %copy.37 = bf16[2,1536,4224]{2,1,0:T(8,128)(2,1)} copy(bf16[2,1536,4224]{2,1,0:T(8,128)(2,1)S(1)} %bitcast.102) | data formatting | bytes 51904512
  542.2 0.0 slice-start.4
  542.2 0.0 slice-start.5
  542.2 0.0 slice-start.6
  542.2 23.5 %copy.38 = bf16[2,1536,4224]{2,1,0:T(8,128)(2,1)} copy(bf16[2,1536,4224]{2,1,0:T(8,128)(2,1)} %bitcast.101) | data formatting | bytes 51904512
  565.8 0.0 slice-done
  565.8 0.0 slice-done.1
  565.8 0.0 slice-done.2
  565.8 0.0 slice-done.3
  565.8 0.0 slice-done.4
  565.8 0.0 slice-done.5
  565.8 0.0 slice-done.6
  565.8 9.2 %copy.39 = bf16[2,4224,1536]{2,1,0:T(8,128)(2,1)} copy(bf16[2,4224,1536]{2,1,0:T(8,128)(2,1)S(1)} %bitcast.100) | data formatting | bytes 51904512
  (1 shorter events, 0.0 us)
Async XLA Ops:
  0.7 1.9 copy-start.1
  511.6 17.4 %copy-start = (bf16[2,16,2,198,8,128]{5,4,3,2,1,0:T(8,128)(2,1)S(1)}, bf16[2,16,2,198,8,128]{5,4,3,2,1,0:T(8,128)(2,1)}, u32[]{:S(2)}) copy-start(bf16[2,16,2,198,8,128]{5,4,3,2,1,0:T(8,128)(2,1)} %get-tuple-element.15) | copy-start | bytes 77856768
  529.0 36.7 %slice-start = ((s8[25952256]{0:T(1024)(128)(4,1)}), s8[4194304]{0:T(1024)(128)(4,1)S(1)}, s32[]{:S(2)}) async-start(s8[25952256]{0:T(1024)(128)(4,1)} %bitcast.98), calls=%async_computation | async-start | bytes 8388608
  529.0 36.7 %slice-start.1 = ((s8[25952256]{0:T(1024)(128)(4,1)}), s8[4194304]{0:T(1024)(128)(4,1)S(1)}, s32[]{:S(2)}) async-start(s8[25952256]{0:T(1024)(128)(4,1)} %bitcast.98), calls=%async_computation.1 | async-start | bytes 8388608
  529.1 36.7 %slice-start.2 = ((s8[25952256]{0:T(1024)(128)(4,1)}), s8[4194304]{0:T(1024)(128)(4,1)S(1)}, s32[]{:S(2)}) async-start(s8[25952256]{0:T(1024)(128)(4,1)} %bitcast.98), calls=%async_computation.2 | async-start | bytes 8388608
  529.1 36.7 %slice-start.3 = ((s8[25952256]{0:T(1024)(128)(4,1)}), s8[4194304]{0:T(1024)(128)(4,1)S(1)}, s32[]{:S(2)}) async-start(s8[25952256]{0:T(1024)(128)(4,1)} %bitcast.98), calls=%async_computation.3 | async-start | bytes 8388608
  542.2 23.6 %slice-start.4 = ((s8[25952256]{0:T(1024)(128)(4,1)}), s8[4194304]{0:T(1024)(128)(4,1)S(1)}, s32[]{:S(2)}) async-start(s8[25952256]{0:T(1024)(128)(4,1)} %bitcast.98), calls=%async_computation.4 | async-start | bytes 8388608
  542.2 23.6 %slice-start.5 = ((s8[25952256]{0:T(1024)(128)(4,1)}), s8[4194304]{0:T(1024)(128)(4,1)S(1)}, s32[]{:S(2)}) async-start(s8[25952256]{0:T(1024)(128)(4,1)} %bitcast.98), calls=%async_computation.5 | async-start | bytes 8388608
  542.2 23.6 %slice-start.6 = ((s8[25952256]{0:T(1024)(128)(4,1)}), s8[786432]{0:T(1024)(128)(4,1)S(1)}, s32[]{:S(2)}) async-start(s8[25952256]{0:T(1024)(128)(4,1)} %bitcast.98), calls=%async_computation.6 | async-start | bytes 1572864
